TPU v7x, 512 devices: a whole 4x8x8 slice. The times are simulated.
512 devices in a mesh: dp: 8 (over x, core), vocab: 64 (over y, z).
Axes of the slice: x: 4, y: 8, z: 8, core: 2. Of those that a mesh axis runs over, the one named last changes fastest.
Arguments:
- hidden: bfloat16 [1792, 4608], P('dp'), may hold values from -15 to 15
- out_weight: bfloat16 [4608, 24576], P('dp', 'vocab'), may hold values from -0.09375 to 0.09375
- targets: int32 [1792], P('dp'), may hold values from 0 to 24383
- token_weight: float32 [1792], P('dp'), may hold values from 0.3 to 3
Outputs:
- token_loss: float32 [1792], P('dp')
- hidden_grad: bfloat16 [1792, 4608], P('dp')
- weight_grad: bfloat16 [4608, 24576], P('dp', 'vocab')
All inputs are finite; a program needn't handle non-finite values.
Results may differ from a plain program's by a relative error of at most 0.0085.
Values may be sent and summed in bfloat16 or wider, within the bound.
A program may use at most 64 MiB of HBM per device.

v0:
```python
import jax
import jax.numpy as jnp
from jax import lax
from jax.sharding import Mesh
from jax.sharding import PartitionSpec as P

VOCAB = ("vocab_0", "vocab_1")
softcap = 30.0


def by_axis(array, axes):
    for axis in axes:
        array = lax.psum(array, axis)
    return array


def in_blocks(array, dim, peers):
    before, after = (array.shape[:dim], array.shape[dim + 1 :])
    return jnp.moveaxis(array.reshape(*before, peers, -1, *after), dim, 0)


def sent_and_summed(array, axis, dim):
    blocks = in_blocks(array, dim, lax.axis_size(axis))
    arrived = lax.all_to_all(blocks, axis, split_axis=0, concat_axis=0, tiled=True)
    return arrived.astype(jnp.float32).sum(axis=0)


def from_everyone(array, axis):
    peers = lax.axis_size(axis)
    return lax.all_to_all(
        jnp.broadcast_to(array[None], (peers, *array.shape)), axis, 0, 0, tiled=True
    )


def in_order(blocks, dim):
    blocks = jnp.moveaxis(blocks, 0, dim)
    lengths = blocks.shape
    return blocks.reshape(*lengths[:dim], lengths[dim] * lengths[dim + 1], *lengths[dim + 2 :])


def gather_directly(array, axis, dim):
    blocks = from_everyone(array, axis)
    return in_order(blocks, dim)


def body(hidden, out_weight, targets, token_weight):
    shard_width = out_weight.shape[1]
    row_count = out_weight.shape[0]
    tok_rows = hidden.shape[0]
    vocab_used = shard_width * lax.axis_size(VOCAB) - shard_width // 2
    first_col = lax.axis_index(VOCAB) * shard_width
    col_ids = first_col + jnp.arange(shard_width, dtype=jnp.int32)
    usable = col_ids < vocab_used
    w_full = lax.all_gather(out_weight, "dp", axis=0, tiled=True)
    logits = jnp.dot(hidden, w_full, preferred_element_type=jnp.float32)
    squash = jnp.tanh(logits / softcap)
    capped = softcap * squash
    exp_terms = jnp.where(usable[None, :], jnp.exp(capped), jnp.float32(0.0))
    target_hit = col_ids[None, :] == targets[:, None]
    local_sum = jnp.sum(exp_terms, axis=1)
    local_target = jnp.sum(jnp.where(target_hit, capped, jnp.float32(0.0)), axis=1)
    sums, target_logit = (by_axis(local_sum, VOCAB), by_axis(local_target, VOCAB))
    token_loss = jnp.log(sums) - target_logit
    onehot = jnp.where(target_hit, jnp.float32(1.0), jnp.float32(0.0))
    logit_grad = (
        token_weight[:, None] * (exp_terms / sums[:, None] - onehot) * (1.0 - squash * squash)
    ).astype(jnp.bfloat16)
    contract_cols = (((1,), (1,)), ((), ()))
    partial_grad = lax.dot_general(
        logit_grad, w_full, contract_cols, preferred_element_type=jnp.float32
    )
    share = sent_and_summed(partial_grad.astype(jnp.bfloat16), VOCAB, 1).astype(jnp.bfloat16)
    hidden_grad = lax.all_gather(share, VOCAB, axis=1, tiled=True)
    owned_cols = lax.all_to_all(hidden, "dp", split_axis=1, concat_axis=0, tiled=True)
    every_grad = gather_directly(logit_grad, "dp", 0)
    block_count = owned_cols.shape[0] // tok_rows
    col_blocks = owned_cols.reshape(block_count, tok_rows, row_count)
    grad_blocks = every_grad.reshape(block_count, tok_rows, shard_width)
    block_terms = jnp.einsum(
        "ntr,ntv->nrv", col_blocks, grad_blocks, preferred_element_type=jnp.float32
    ).astype(jnp.bfloat16)
    weight_grad = jnp.sum(block_terms.astype(jnp.float32), axis=0).astype(jnp.bfloat16)
    return (token_loss, hidden_grad, weight_grad)


def solution(mesh):
    torus = Mesh(mesh.devices.reshape(mesh.shape["dp"], 8, 8), ("dp", "vocab_0", "vocab_1"))
    in_specs = (P("dp", None), P("dp", VOCAB), P("dp"), P("dp"))
    out_specs = (P("dp"), P("dp", None), P("dp", VOCAB))
    return jax.shard_map(body, mesh=torus, in_specs=in_specs, out_specs=out_specs, check_vma=False)
```

profile of v0, /device:TPU:4, one launch (start us, length us, event | category | flops | bytes accessed | tf_op | source)
XLA Modules:
  0.0 244.0 jit_solution(11273807396610826851)
XLA Ops:
  7.2 0.0 all-gather.3.cloned.1.call-start
  7.2 0.7 all-gather.3.cloned.1.call-update
  7.9 0.0 all-gather.5.cloned.1.call-start
  8.0 0.0 copy-start
  8.0 0.0 copy-start.1
  8.0 40.0 %all-gather.3.cloned.1.call-done = bf16[4608,384]{1,0:T(8,128)(2,1)} async-done(((bf16[576,384]{1,0:T(8,128)(2,1)}), bf16[4608,384]{1,0:T(8,128)(2,1)}) %all-gather.3.cloned.1.call-update) | async-done | bytes 3538960 | tf_op jit(solution)/shard_map/all_gather | solution.py:54
  48.0 4.1 %fusion.7 = (f32[224]{0:T(256)S(1)}, f32[224]{0:T(256)S(1)}, f32[224,384]{1,0:T(8,128)S(1)}) fusion(pred[384]{0:T(512)(128)(4,1)S(1)} %broadcast_compare_fusion, s32[224]{0:T(256)} %param.6, s32[384]{0:T(512)S(1)} %iota_add_fusion, bf16[224,4608]{1,0:T(8,128)(2,1)} %param.4, bf16[4608,384]{1,0:T(8,128)(2,1)} %all-gather.3.cloned.1.call-done), kind=kOutput, calls=%fused_computation.13 | convolution fusion | flops 793325056 | bytes 5952000 | tf_op jit(solution)/shard_map/dot_general | solution.py:55
  52.1 17.0 %all-reduce.1 = (f32[224]{0:T(256)S(1)}, f32[224]{0:T(256)S(1)}) all-reduce(f32[224]{0:T(256)S(1)} %get-tuple-element.7, f32[224]{0:T(256)S(1)} %get-tuple-element.6), channel_id=1, replica_groups=mesh['dp'=8,'vocab_0'=8,'vocab_1'=8] {'vocab_0'}, use_global_device_ids=true, to_apply=%region_4.5 | all-reduce | flops 448 | bytes 3584 | tf_op jit(solution)/shard_map/psum | solution.py:13
  69.1 18.1 %all-reduce = (f32[224]{0:T(256)S(1)}, f32[224]{0:T(256)S(1)}) all-reduce(f32[224]{0:T(256)S(1)} %get-tuple-element.10, f32[224]{0:T(256)S(1)} %get-tuple-element.11), channel_id=1, replica_groups=mesh['dp'=8,'vocab_0'=8,'vocab_1'=8] {'vocab_1'}, use_global_device_ids=true, to_apply=%region_5.6 | all-reduce | flops 448 | bytes 3584 | tf_op jit(solution)/shard_map/psum | solution.py:13
  87.2 0.0 copy-done
  87.2 0.0 copy-done.1
  87.2 0.2 fusion.6
  87.4 3.4 %convolution_convert_fusion = bf16[224,4608]{1,0:T(8,128)(2,1)S(1)} fusion(bf16[224,384]{1,0:T(8,128)(2,1)S(1)} %fusion.6, bf16[4608,384]{1,0:T(8,128)(2,1)} %all-gather.3.cloned.1.call-done), kind=kOutput, calls=%fused_computation | convolution fusion | flops 793755648 | bytes 5775360 | tf_op jit(solution)/shard_map/dot_general | solution.py:69
  90.8 2.4 copy.9
  93.2 60.9 %all_to_all.26 = bf16[64,224,72]{1,2,0:T(8,128)(2,1)S(1)} all-to-all(bf16[64,224,72]{1,2,0:T(8,128)(2,1)} %bitcast.12), channel_id=1, replica_groups=mesh['dp'=8,'vocab_0'=8,'vocab_1'=8] {'vocab_0','vocab_1'}, dimensions={0} | all-to-all | bytes 4128768 | tf_op jit(solution)/shard_map/all_to_all | solution.py:24
  154.1 1.0 reduce_sum.46
  155.1 0.0 all-gather.5.cloned.1.call-update
  155.1 3.6 %all_to_all.20 = bf16[224,8,576]{2,1,0:T(8,128)(2,1)S(1)} reshape(bf16[224,4608]{1,0:T(8,128)(2,1)} %param.4) | data formatting | bytes 4128768 | tf_op jit(solution)/shard_map/all_to_all | solution.py:74
  158.7 0.3 copy.10
  159.0 31.3 %all_to_all.27 = bf16[224,8,576]{2,0,1:T(8,128)(2,1)S(1)} all-to-all(bf16[224,8,576]{2,0,1:T(8,128)(2,1)S(1)} %copy.10), channel_id=1, replica_groups=mesh['dp'=8,'vocab_0'=8,'vocab_1'=8] {'dp'}, dimensions={1} | all-to-all | bytes 4128768 | tf_op jit(solution)/shard_map/all_to_all | solution.py:74
  190.2 1.2 broadcast_in_dim.34
  191.4 6.8 %all-to-all-start.1 = ((bf16[8,224,384]{2,1,0:T(8,128)(2,1)}), bf16[8,224,384]{2,1,0:T(8,128)(2,1)}, u32[]{:S(2)}, u32[]{:S(2)}) async-start(bf16[8,224,384]{2,1,0:T(8,128)(2,1)} %broadcast_in_dim.34), calls=%async_computation.1 | async-start | bytes 2752512 | tf_op jit(solution)/shard_map/all_to_all | solution.py:30
  198.3 0.6 log_subtract_fusion
  198.8 15.8 %all-to-all-done.1 = bf16[8,224,384]{2,1,0:T(8,128)(2,1)} async-done(((bf16[8,224,384]{2,1,0:T(8,128)(2,1)}), bf16[8,224,384]{2,1,0:T(8,128)(2,1)}, u32[]{:S(2)}, u32[]{:S(2)}) %all-to-all-start.1) | async-done | bytes 1376288 | tf_op jit(solution)/shard_map/all_to_all | solution.py:30
  214.7 3.6 %convert_reduce_fusion = bf16[384,576]{0,1:T(8,128)(2,1)} fusion(bf16[8,224,384]{2,1,0:T(8,128)(2,1)} %all-to-all-done.1, bf16[224,8,576]{2,0,1:T(8,128)(2,1)S(1)} %all_to_all.27), kind=kOutput, calls=%fused_computation.1 | convolution fusion | flops 796041216 | bytes 3883008 | tf_op jit(solution)/shard_map/ntr,ntv->nrv/dot_general | solution.py:79
  218.3 14.7 %all-gather.5.cloned.1.call-done = bf16[224,4608]{0,1:T(8,128)(2,1)} async-done(((bf16[224,72]{0,1:T(8,128)(2,1)}), bf16[224,4608]{0,1:T(8,128)(2,1)}) %all-gather.5.cloned.1.call-update) | async-done | bytes 2064400 | tf_op jit(solution)/shard_map/all_gather | solution.py:73
  233.0 4.1 %copy.11 = bf16[224,4608]{1,0:T(8,128)(2,1)} copy(bf16[224,4608]{0,1:T(8,128)(2,1)} %all-gather.5.cloned.1.call-done) | data formatting | bytes 4128768
  (2 shorter events, 0.0 us)
Async XLA Ops:
  7.2 40.9 %all-gather.3.cloned.1.call-start = ((), (), s32[]{:S(2)}) async-start(), calls=%async_computation.3 | async-start | bytes 3981312 | tf_op jit(solution)/shard_map/all_gather | solution.py:54
  7.9 225.1 %all-gather.5.cloned.1.call-start = ((), (), s32[]{:S(2)}) async-start(), calls=%async_computation.4 | async-start | bytes 2396160 | tf_op jit(solution)/shard_map/all_gather | solution.py:73
  8.0 79.2 %copy-start = (s32[224]{0:T(256)S(1)}, s32[224]{0:T(256)}, u32[]{:S(2)}) copy-start(s32[224]{0:T(256)} %param.6) | copy-start | bytes 2692
  8.0 79.2 %copy-start.1 = (f32[224]{0:T(256)S(1)}, f32[224]{0:T(256)}, u32[]{:S(2)}) copy-start(f32[224]{0:T(256)} %param.7) | copy-start | bytes 2692
  191.4 23.2 %all-to-all-start.1 = ((bf16[8,224,384]{2,1,0:T(8,128)(2,1)}), bf16[8,224,384]{2,1,0:T(8,128)(2,1)}, u32[]{:S(2)}, u32[]{:S(2)}) async-start(bf16[8,224,384]{2,1,0:T(8,128)(2,1)} %broadcast_in_dim.34), calls=%async_computation.1 | async-start | bytes 2752512 | tf_op jit(solution)/shard_map/all_to_all | solution.py:30
Sparse Core Ops, SparseCore 0:
  10.1 37.8 all-gather.2
  155.2 77.6 all-gather.4
where the time goes:
time: 244 us
  blocking collectives  127 us (52%)
  waiting for transfers between devices  71.2 us (29%)
  between operations  14.1 us (6%)
  local copies, waits for them, and re-layouts  11.6 us (5%)
  matrix products  11.1 us (5%)
  starting transfers between devices  6.9 us (3%)
    all_to_all x1, blocking collectives, sent_and_summed(): lax.all_to_all(blocks, axis, split_axis=0, concat_axis=0, tiled=True)  60.9 us
    all_gather x1, waiting for transfers between devices, body(): w_full = lax.all_gather(out_weight, 'dp', axis=0, tiled=True)  40 us
    psum x2, blocking collectives, by_axis(): array = lax.psum(array, axis)  35.1 us
    all_to_all x1, blocking collectives, body(): lax.all_to_all(hidden, 'dp', split_axis=1, concat_axis=0, tiled=True)  31.3 us
    all_to_all x1, waiting for transfers between devices, from_everyone(): lax.all_to_all(jnp.broadcast_to(array[None], (peers, *array.shape)), axis...  15.8 us
    all_gather x1, waiting for transfers between devices, body(): hidden_grad = lax.all_gather(share, VOCAB, axis=1, tiled=True)  14.7 us
    all_to_all x1, starting transfers between devices, from_everyone(): lax.all_to_all(jnp.broadcast_to(array[None], (peers, *array.shape)), axis...  6.83 us
  transfers between devices with their start and end apart: 3, of which 3 were waited for; matrix products, arithmetic and copies ran while one was open for 2% of the time, Pallas kernels for 0%

commit v1 on v0

--- a/solution.py
+++ b/solution.py
@@ -70,7 +70,9 @@
         logit_grad, w_full, contract_cols, preferred_element_type=jnp.float32
     )
     share = sent_and_summed(partial_grad.astype(jnp.bfloat16), VOCAB, 1).astype(jnp.bfloat16)
-    hidden_grad = lax.all_gather(share, VOCAB, axis=1, tiled=True)
+    hidden_grad = jnp.concatenate(
+        lax.all_to_all(jnp.stack([share] * lax.axis_size(VOCAB)), VOCAB, 0, 0), axis=1
+    )
     owned_cols = lax.all_to_all(hidden, "dp", split_axis=1, concat_axis=0, tiled=True)
     every_grad = gather_directly(logit_grad, "dp", 0)
     block_count = owned_cols.shape[0] // tok_rows

time: 244 us -> 271 us (1.11)
  the two profiles are of different devices: /device:TPU:4 before, /device:TPU:8 now
where the time goes in v1:
time: 271 us
  waiting for transfers between devices  120 us (44%)
  blocking collectives  95.4 us (35%)
  starting transfers between devices  16.1 us (6%)
  between operations  14.1 us (5%)
  local copies, waits for them, and re-layouts  12.8 us (5%)
  matrix products  11.2 us (4%)
    all_to_all x1, blocking collectives, sent_and_summed(): lax.all_to_all(blocks, axis, split_axis=0, concat_axis=0, tiled=True)  60.6 us
    all_to_all x1, waiting for transfers between devices, body(): lax.all_to_all(jnp.stack([share] * lax.axis_size(VOCAB)), VOCAB, 0, 0)  55.6 us
    all_gather x1, waiting for transfers between devices, body(): w_full = lax.all_gather(out_weight, 'dp', axis=0, tiled=True)  44.7 us
    psum x2, blocking collectives, by_axis(): array = lax.psum(array, axis)  34.8 us
    all_to_all x1, waiting for transfers between devices, from_everyone(): lax.all_to_all(jnp.broadcast_to(array[None], (peers, *array.shape)), axis...  19 us
    all_to_all x1, starting transfers between devices, body(): lax.all_to_all(jnp.stack([share] * lax.axis_size(VOCAB)), VOCAB, 0, 0)  7.29 us
  transfers between devices with their start and end apart: 4, of which 3 were waited for; matrix products, arithmetic and copies ran while one was open for 6% of the time, Pallas kernels for 0%

profile of v1, /device:TPU:8, one launch (start us, length us, event | category | flops | bytes accessed | tf_op | source)
XLA Modules:
  0.0 270.7 jit_solution(12100633851488717122)
XLA Ops:
  7.2 0.0 all-gather.2.cloned.1.call-start
  7.2 0.7 all-gather.2.cloned.1.call-update
  7.9 3.6 %all_to_all.24 = bf16[224,8,576]{2,1,0:T(8,128)(2,1)S(1)} reshape(bf16[224,4608]{1,0:T(8,128)(2,1)} %param.4) | data formatting | bytes 4128768 | tf_op jit(solution)/shard_map/all_to_all | solution.py:76
  11.5 1.7 copy.8
  13.1 0.0 copy-start
  13.1 0.0 copy-start.1
  13.1 4.5 %all-to-all-start.3 = ((bf16[224,8,576]{2,0,1:T(8,128)(2,1)}), bf16[224,8,576]{2,0,1:T(8,128)(2,1)}, u32[]{:S(2)}, u32[]{:S(2)}) async-start(bf16[224,8,576]{2,0,1:T(8,128)(2,1)} %copy.8), calls=%async_computation.3 | async-start | bytes 4587520 | tf_op jit(solution)/shard_map/all_to_all | solution.py:76
  17.6 0.0 copy-start.2
  17.7 44.7 %all-gather.2.cloned.1.call-done = bf16[4608,384]{1,0:T(8,128)(2,1)} async-done(((bf16[576,384]{1,0:T(8,128)(2,1)}), bf16[4608,384]{1,0:T(8,128)(2,1)}) %all-gather.2.cloned.1.call-update) | async-done | bytes 3538960 | tf_op jit(solution)/shard_map/all_gather | solution.py:54
  62.4 0.0 copy-done
  62.4 0.0 copy-done.1
  62.4 3.4 %fusion.7 = (f32[224]{0:T(256)S(1)}, f32[224]{0:T(256)S(1)}, f32[224,384]{1,0:T(8,128)S(1)}) fusion(pred[384]{0:T(512)(128)(4,1)S(1)} %broadcast_compare_fusion, s32[224]{0:T(256)S(1)} %copy-done.1, s32[384]{0:T(512)S(1)} %iota_add_fusion, bf16[224,4608]{1,0:T(8,128)(2,1)S(1)} %copy-done, bf16[4608,384]{1,0:T(8,128)(2,1)} %all-gather.2.cloned.1.call-done), kind=kOutput, calls=%fused_computation.13 | convolution fusion | flops 793325056 | bytes 5952000 | tf_op jit(solution)/shard_map/dot_general | solution.py:55
  65.8 16.1 %all-reduce.1 = (f32[224]{0:T(256)S(1)}, f32[224]{0:T(256)S(1)}) all-reduce(f32[224]{0:T(256)S(1)} %get-tuple-element.7, f32[224]{0:T(256)S(1)} %get-tuple-element.6), channel_id=1, replica_groups=mesh['dp'=8,'vocab_0'=8,'vocab_1'=8] {'vocab_0'}, use_global_device_ids=true, to_apply=%region_4.5 | all-reduce | flops 448 | bytes 3584 | tf_op jit(solution)/shard_map/psum | solution.py:13
  81.9 18.6 %all-reduce = (f32[224]{0:T(256)S(1)}, f32[224]{0:T(256)S(1)}) all-reduce(f32[224]{0:T(256)S(1)} %get-tuple-element.10, f32[224]{0:T(256)S(1)} %get-tuple-element.11), channel_id=1, replica_groups=mesh['dp'=8,'vocab_0'=8,'vocab_1'=8] {'vocab_1'}, use_global_device_ids=true, to_apply=%region_5.6 | all-reduce | flops 448 | bytes 3584 | tf_op jit(solution)/shard_map/psum | solution.py:13
  100.5 0.0 copy-done.2
  100.5 0.2 fusion.6
  100.7 3.4 %convolution_convert_fusion = bf16[224,4608]{1,0:T(8,128)(2,1)S(1)} fusion(bf16[224,384]{1,0:T(8,128)(2,1)S(1)} %fusion.6, bf16[4608,384]{1,0:T(8,128)(2,1)} %all-gather.2.cloned.1.call-done), kind=kOutput, calls=%fused_computation | convolution fusion | flops 793755648 | bytes 5775360 | tf_op jit(solution)/shard_map/dot_general | solution.py:69
  104.1 2.4 copy.7
  106.6 0.0 all-to-all-done.3
  106.6 60.6 %all_to_all.31 = bf16[64,224,72]{1,2,0:T(8,128)(2,1)S(1)} all-to-all(bf16[64,224,72]{1,2,0:T(8,128)(2,1)} %bitcast.16), channel_id=1, replica_groups=mesh['dp'=8,'vocab_0'=8,'vocab_1'=8] {'vocab_0','vocab_1'}, dimensions={0} | all-to-all | bytes 4128768 | tf_op jit(solution)/shard_map/all_to_all | solution.py:24
  167.2 1.2 broadcast_in_dim.34
  168.4 4.3 %all-to-all-start.2 = ((bf16[8,224,384]{2,1,0:T(8,128)(2,1)}), bf16[8,224,384]{2,1,0:T(8,128)(2,1)}, u32[]{:S(2)}, u32[]{:S(2)}) async-start(bf16[8,224,384]{2,1,0:T(8,128)(2,1)} %broadcast_in_dim.34), calls=%async_computation.2 | async-start | bytes 2752512 | tf_op jit(solution)/shard_map/all_to_all | solution.py:30
  172.7 0.4 reduce_sum.46
  173.1 19.0 %all-to-all-done.2 = bf16[8,224,384]{2,1,0:T(8,128)(2,1)} async-done(((bf16[8,224,384]{2,1,0:T(8,128)(2,1)}), bf16[8,224,384]{2,1,0:T(8,128)(2,1)}, u32[]{:S(2)}, u32[]{:S(2)}) %all-to-all-start.2) | async-done | bytes 1376288 | tf_op jit(solution)/shard_map/all_to_all | solution.py:30
  192.2 1.6 stack.2
  193.7 7.3 %all-to-all-start.1 = ((bf16[64,224,72]{1,2,0:T(8,128)(2,1)}), bf16[64,224,72]{1,2,0:T(8,128)(2,1)S(1)}, u32[]{:S(2)}, u32[]{:S(2)}) async-start(bf16[64,224,72]{1,2,0:T(8,128)(2,1)} %stack.2), calls=%async_computation.1 | async-start | bytes 4718592 | tf_op jit(solution)/shard_map/all_to_all | solution.py:74
  201.0 0.6 log_subtract_fusion
  201.6 4.4 %convert_reduce_fusion = bf16[384,576]{0,1:T(8,128)(2,1)} fusion(bf16[8,224,384]{2,1,0:T(8,128)(2,1)} %all-to-all-done.2, bf16[224,8,576]{2,0,1:T(8,128)(2,1)} %all-to-all-done.3), kind=kOutput, calls=%fused_computation.1 | convolution fusion | flops 796041216 | bytes 3883008 | tf_op jit(solution)/shard_map/ntr,ntv->nrv/dot_general | solution.py:81
  206.0 55.6 %all-to-all-done.1 = bf16[64,224,72]{1,2,0:T(8,128)(2,1)S(1)} async-done(((bf16[64,224,72]{1,2,0:T(8,128)(2,1)}), bf16[64,224,72]{1,2,0:T(8,128)(2,1)S(1)}, u32[]{:S(2)}, u32[]{:S(2)}) %all-to-all-start.1) | async-done | bytes 2064416 | tf_op jit(solution)/shard_map/all_to_all | solution.py:74
  261.5 2.3 copy.9
  (2 shorter events, 0.0 us)
Async XLA Ops:
  7.2 55.2 %all-gather.2.cloned.1.call-start = ((), (), s32[]{:S(2)}) async-start(), calls=%async_computation.4 | async-start | bytes 3981312 | tf_op jit(solution)/shard_map/all_gather | solution.py:54
  13.1 49.2 %copy-start = (bf16[224,4608]{1,0:T(8,128)(2,1)S(1)}, bf16[224,4608]{1,0:T(8,128)(2,1)}, u32[]{:S(2)}) copy-start(bf16[224,4608]{1,0:T(8,128)(2,1)} %param.4) | copy-start | bytes 6193156
  13.1 49.2 %copy-start.1 = (s32[224]{0:T(256)S(1)}, s32[224]{0:T(256)}, u32[]{:S(2)}) copy-start(s32[224]{0:T(256)} %param.6) | copy-start | bytes 2692
  13.1 93.5 %all-to-all-start.3 = ((bf16[224,8,576]{2,0,1:T(8,128)(2,1)}), bf16[224,8,576]{2,0,1:T(8,128)(2,1)}, u32[]{:S(2)}, u32[]{:S(2)}) async-start(bf16[224,8,576]{2,0,1:T(8,128)(2,1)} %copy.8), calls=%async_computation.3 | async-start | bytes 4587520 | tf_op jit(solution)/shard_map/all_to_all | solution.py:76
  17.6 82.9 %copy-start.2 = (f32[224]{0:T(256)S(1)}, f32[224]{0:T(256)}, u32[]{:S(2)}) copy-start(f32[224]{0:T(256)} %param.7) | copy-start | bytes 2692
  168.4 23.7 %all-to-all-start.2 = ((bf16[8,224,384]{2,1,0:T(8,128)(2,1)}), bf16[8,224,384]{2,1,0:T(8,128)(2,1)}, u32[]{:S(2)}, u32[]{:S(2)}) async-start(bf16[8,224,384]{2,1,0:T(8,128)(2,1)} %broadcast_in_dim.34), calls=%async_computation.2 | async-start | bytes 2752512 | tf_op jit(solution)/shard_map/all_to_all | solution.py:30
  193.7 67.8 %all-to-all-start.1 = ((bf16[64,224,72]{1,2,0:T(8,128)(2,1)}), bf16[64,224,72]{1,2,0:T(8,128)(2,1)S(1)}, u32[]{:S(2)}, u32[]{:S(2)}) async-start(bf16[64,224,72]{1,2,0:T(8,128)(2,1)} %stack.2), calls=%async_computation.1 | async-start | bytes 4718592 | tf_op jit(solution)/shard_map/all_to_all | solution.py:74
Sparse Core Ops, SparseCore 0:
  10.1 52.2 all-gather.1
